TPU v7x, 32 devices: a whole 2x2x4 slice. The times are simulated.
32 devices in a mesh: row: 16 (over z, y, core), col: 2 (over x).
Axes of the slice: x: 2, y: 2, z: 4, core: 2. Of those that a mesh axis runs over, the one named last changes fastest.
Arguments:
- pair_act: bfloat16 [192, 192, 128], P('row', 'col'), may hold values from -6 to 6
- tile_mask: int32 [12, 12], replicated, may hold values 0 or 1
- w_left_gate: bfloat16 [128, 128], replicated, may hold values from -0.5 to 0.5
- w_left: bfloat16 [128, 128], replicated, may hold values from -0.5 to 0.5
- w_right_gate: bfloat16 [128, 128], replicated, may hold values from -0.5 to 0.5
- w_right: bfloat16 [128, 128], replicated, may hold values from -0.5 to 0.5
- w_out_gate: bfloat16 [128, 128], replicated, may hold values from -0.5 to 0.5
- w_out: bfloat16 [128, 128], replicated, may hold values from -0.5 to 0.5
Outputs:
- update: bfloat16 [192, 192, 128], P('row', 'col')
All inputs are finite; a program needn't handle non-finite values.
Results may differ from a plain program's by a relative error of at most 0.0083.
Values may be sent and summed in bfloat16 or wider, within the bound.
A program may use at most 64 MiB of HBM per device.

v0:
```python
import functools

import jax
import jax.numpy as jnp
from jax import lax
from jax.experimental import pallas as pl
from jax.experimental.pallas import tpu as pltpu
from jax.sharding import PartitionSpec as P

TILES = 12
GROUP = 8
MESH = pl.DeviceIdType.MESH


def norm_axis(values, axis):
    mean = jnp.mean(values, axis=axis, keepdims=True)
    centred = values - mean
    spread = jnp.mean(centred * centred, axis=axis, keepdims=True)
    return centred * lax.rsqrt(spread + 1e-05)


def place(flat, col_size):
    return (flat // col_size, flat % col_size)


def greet(flat, first, count, col_size):
    barrier = pltpu.get_barrier_semaphore()

    def signal(step, _):
        other = first + (flat - first + step) % count
        pl.semaphore_signal(barrier, inc=1, device_id=place(other, col_size), device_id_type=MESH)
        return 0

    lax.fori_loop(1, count, signal, 0)
    pl.semaphore_wait(barrier, count - 1)


def spread_kernel(
    sizes, left, right, left_all, right_all, own_sem, left_send, left_recv, right_send, right_recv
):
    row_size, col_size, groups = sizes
    devices = row_size * col_size
    flat = lax.axis_index("row") * col_size + lax.axis_index("col")
    member = flat % groups
    first = flat - member

    def chunk(source, group):
        return source.at[group]

    own_left = pltpu.make_async_copy(chunk(left, member), left_all.at[member], own_sem.at[0])
    own_right = pltpu.make_async_copy(chunk(right, member), right_all.at[flat], own_sem.at[1])
    own_left.start()
    own_right.start()
    greet(flat, 0, devices, col_size)

    def right_copy(step):
        to = (flat + step) % devices
        return pltpu.make_async_remote_copy(
            src_ref=chunk(right, to % groups),
            dst_ref=right_all.at[flat],
            send_sem=right_send.at[step],
            recv_sem=right_recv.at[step],
            device_id=place(to, col_size),
            device_id_type=MESH,
        )

    def left_copy(step):
        to = (member + step) % groups
        return pltpu.make_async_remote_copy(
            src_ref=chunk(left, to),
            dst_ref=left_all.at[member],
            send_sem=left_send.at[step],
            recv_sem=left_recv.at[step],
            device_id=place(first + to, col_size),
            device_id_type=MESH,
        )

    def start_right(step, _):
        right_copy(step).start()
        return 0

    def start_left(step, _):
        left_copy(step).start()
        return 0

    def wait_right(step, _):
        right_copy(step).wait()
        return 0

    def wait_left(step, _):
        left_copy(step).wait()
        return 0

    lax.fori_loop(1, devices, start_right, 0)
    lax.fori_loop(1, groups, start_left, 0)
    own_left.wait()
    own_right.wait()
    lax.fori_loop(1, groups, wait_left, 0)
    lax.fori_loop(1, devices, wait_right, 0)


def return_kernel(sizes, triangle, owned, own_sem, send, recv):
    row_size, col_size, groups = sizes
    flat = lax.axis_index("row") * col_size + lax.axis_index("col")
    member = flat % groups
    first = flat - member
    own = pltpu.make_async_copy(triangle.at[member], owned.at[member], own_sem)
    own.start()
    greet(flat, first, groups, col_size)

    def copy(step):
        to = (member + step) % groups
        return pltpu.make_async_remote_copy(
            src_ref=triangle.at[to],
            dst_ref=owned.at[member],
            send_sem=send.at[step],
            recv_sem=recv.at[step],
            device_id=place(first + to, col_size),
            device_id_type=MESH,
        )

    def start(step, _):
        copy(step).start()
        return 0

    def wait(step, _):
        copy(step).wait()
        return 0

    lax.fori_loop(1, groups, start, 0)
    own.wait()
    lax.fori_loop(1, groups, wait, 0)


def local(
    sizes, pair_act, tile_mask, w_left_gate, w_left, w_right_gate, w_right, w_out_gate, w_out
):
    row_size, col_size, groups = sizes
    devices = row_size * col_size
    block_rows = groups // col_size
    rows, cols, width = pair_act.shape
    residues = rows * row_size
    tile = residues // TILES
    normed = norm_axis(pair_act.astype(jnp.float32), 2).astype(jnp.bfloat16)
    tile_range = lax.iota(jnp.int32, TILES)
    row_ids = (lax.axis_index("row") * rows + lax.iota(jnp.int32, rows)) // tile
    col_ids = (lax.axis_index("col") * cols + lax.iota(jnp.int32, cols)) // tile
    row_hot = (row_ids[:, None] == tile_range[None, :]).astype(jnp.float32)
    col_hot = (col_ids[:, None] == tile_range[None, :]).astype(jnp.float32)
    pair_mask = jnp.dot(
        jnp.dot(row_hot, tile_mask.astype(jnp.float32), preferred_element_type=jnp.float32),
        col_hot.T,
        preferred_element_type=jnp.float32,
    )
    pairs = rows * cols
    flat_normed = normed.reshape(pairs, width)
    flat_mask = pair_mask.reshape(1, pairs)

    def project(weight):
        return jnp.einsum("pd,de->ep", flat_normed, weight, preferred_element_type=jnp.float32)

    def factor(gate, value):
        out = jax.nn.sigmoid(project(gate)) * project(value) * flat_mask
        return out.astype(jnp.bfloat16).reshape(groups, GROUP, pairs)

    left = factor(w_left_gate, w_left)
    right = factor(w_right_gate, w_right)
    anywhere = pl.BlockSpec(memory_space=pl.ANY)
    left_all, right_all = pl.pallas_call(
        functools.partial(spread_kernel, sizes),
        out_shape=(
            jax.ShapeDtypeStruct((groups, GROUP, pairs), jnp.bfloat16),
            jax.ShapeDtypeStruct((devices, GROUP, pairs), jnp.bfloat16),
        ),
        in_specs=[anywhere] * 2,
        out_specs=(anywhere, anywhere),
        scratch_shapes=[
            pltpu.SemaphoreType.DMA((2,)),
            pltpu.SemaphoreType.DMA((groups,)),
            pltpu.SemaphoreType.DMA((groups,)),
            pltpu.SemaphoreType.DMA((devices,)),
            pltpu.SemaphoreType.DMA((devices,)),
        ],
        compiler_params=pltpu.CompilerParams(collective_id=0, has_side_effects=True),
    )(left, right)
    left_rows = (
        left_all.reshape(block_rows, col_size, GROUP, rows, cols)
        .transpose(2, 0, 3, 1, 4)
        .reshape(GROUP, block_rows * rows, residues)
    )
    right_rows = (
        right_all.reshape(row_size, col_size, GROUP, rows, cols)
        .transpose(2, 0, 3, 1, 4)
        .reshape(GROUP, residues, residues)
    )
    triangle = jnp.einsum(
        "cik,cjk->cij", left_rows, right_rows, preferred_element_type=jnp.float32
    ).astype(jnp.bfloat16)
    triangle = (
        triangle.reshape(GROUP, block_rows, rows, col_size, cols)
        .transpose(1, 3, 0, 2, 4)
        .reshape(groups, GROUP, pairs)
    )
    owned = pl.pallas_call(
        functools.partial(return_kernel, sizes),
        out_shape=jax.ShapeDtypeStruct((groups, GROUP, pairs), jnp.bfloat16),
        in_specs=[anywhere],
        out_specs=anywhere,
        scratch_shapes=[
            pltpu.SemaphoreType.DMA,
            pltpu.SemaphoreType.DMA((groups,)),
            pltpu.SemaphoreType.DMA((groups,)),
        ],
        compiler_params=pltpu.CompilerParams(collective_id=1, has_side_effects=True),
    )(triangle)
    owned = owned.reshape(width, pairs)
    scaled = norm_axis(owned.astype(jnp.float32), 0).astype(jnp.bfloat16)
    projected = jnp.einsum("cp,ce->pe", scaled, w_out, preferred_element_type=jnp.float32)
    gate = jax.nn.sigmoid(
        jnp.einsum("pd,de->pe", flat_normed, w_out_gate, preferred_element_type=jnp.float32)
    )
    return (gate * projected).astype(jnp.bfloat16).reshape(rows, cols, width)


LANES = 128


def fused_kernel(
    sizes, shape, pair_in, tiles_in, *rest
):
    weights_in, out = rest[:6], rest[6]
    (
        pair, tiles, w_left_gate, w_left, w_right_gate, w_right, w_out_gate, w_out, input_sem, made_out, out_sem,
        normed, gate, left, right, left_all, right_all, left_mat, right_mat, left_lines, product, triangle, owned,
        left_send, left_recv, right_send, right_recv, back_send, back_recv,
    ) = rest[7:]
    kept = (pair, tiles, w_left_gate, w_left, w_right_gate, w_right, w_out_gate, w_out)
    fetches = [
        pltpu.make_async_copy(source, target, input_sem.at[index])
        for index, (source, target) in enumerate(zip((pair_in, tiles_in, *weights_in), kept))
    ]
    row_size, col_size, groups = sizes
    rows, cols, width = shape
    devices = row_size * col_size
    blocks = devices // groups
    block_rows = groups // col_size
    pairs = rows * cols
    tile = rows * row_size // TILES
    row, col = lax.axis_index("row"), lax.axis_index("col")
    flat = row * col_size + col
    member = flat % groups
    block = flat // groups
    first = block * groups

    barrier = pltpu.get_barrier_semaphore()

    def signal(step, _):
        pl.semaphore_signal(
            barrier, inc=1, device_id=place((flat + step) % devices, col_size), device_id_type=MESH
        )
        return 0

    fetches[0].start()
    lax.fori_loop(1, devices, signal, 0)
    for fetch in fetches[1:]:
        fetch.start()
    fetches[0].wait()

    values = pair[...].astype(jnp.float32)
    normed[...] = norm_axis(values, 1).astype(jnp.bfloat16)

    for fetch in fetches[1:]:
        fetch.wait()
    spot = lax.broadcasted_iota(jnp.int32, (1, pairs), 1)
    within = spot
    for line in range(1, rows):
        within = jnp.where(spot >= line * cols, spot - line * cols, within)
    tile_ids = lax.broadcasted_iota(jnp.int32, (TILES, pairs), 0)
    row_low = (tile_ids * tile - row * rows) * cols
    row_hot = ((spot >= row_low) & (spot < row_low + tile * cols)).astype(jnp.float32)
    col_low = tile_ids * tile - col * cols
    col_hot = ((within >= col_low) & (within < col_low + tile)).astype(jnp.float32)
    picked = jnp.dot(tiles[...].astype(jnp.float32).T, row_hot, preferred_element_type=jnp.float32)
    mask = jnp.sum(picked * col_hot, axis=0, keepdims=True)

    def project(weight):
        turned = weight[...].astype(jnp.float32).T.astype(jnp.bfloat16)
        return lax.dot_general(
            turned, normed[...], (((1,), (1,)), ((), ())), preferred_element_type=jnp.float32
        )

    def factor(gate_weight, weight, target):
        made = jax.nn.sigmoid(project(gate_weight)) * project(weight) * mask
        for group in range(groups):
            target[group] = made[group * GROUP : (group + 1) * GROUP].astype(jnp.bfloat16)

    def right_copy(ahead, step):
        to = (member + step) % groups
        return pltpu.make_async_remote_copy(
            src_ref=right.at[to],
            dst_ref=right_all.at[flat],
            send_sem=right_send.at[ahead * groups + step],
            recv_sem=right_recv.at[ahead * groups + step],
            device_id=place((block + ahead) % blocks * groups + to, col_size),
            device_id_type=MESH,
        )

    def member_copy(source, target, send, recv, step):
        to = (member + step) % groups
        return pltpu.make_async_remote_copy(
            src_ref=source.at[to],
            dst_ref=target.at[member],
            send_sem=send.at[step],
            recv_sem=recv.at[step],
            device_id=place(first + to, col_size),
            device_id_type=MESH,
        )

    def left_copy(step):
        return member_copy(left, left_all, left_send, left_recv, step)

    def back_copy(to, slot):
        return pltpu.make_async_remote_copy(
            src_ref=triangle.at[to],
            dst_ref=owned.at[slot],
            send_sem=back_send.at[to],
            recv_sem=back_recv.at[slot],
            device_id=place(first + to, col_size),
            device_id_type=MESH,
        )

    def each(start, stop, do):
        def body(step, _):
            do(step)
            return 0

        lax.fori_loop(start, stop, body, 0)

    factor(w_right_gate, w_right, right)
    factor(w_left_gate, w_left, left)
    pl.semaphore_wait(barrier, devices - 1)
    each(1, groups, lambda step: right_copy(0, step).start())
    each(1, groups, lambda step: left_copy(step).start())
    for ahead in range(1, blocks):
        each(0, groups, lambda step: right_copy(ahead, step).start())

    gate[...] = jax.nn.sigmoid(
        jnp.dot(normed[...], w_out_gate[...], preferred_element_type=jnp.float32)
    )
    left_mat[...] = jnp.zeros_like(left_mat)
    right_mat[...] = jnp.zeros_like(right_mat)
    lane = lax.broadcasted_iota(jnp.int32, (GROUP, LANES), 1)

    def spread(chunk, target, half, start):
        parts = [
            chunk[:, at : at + LANES].astype(jnp.float32) for at in range(0, pairs, LANES)
        ]
        for line in range(rows):
            at, off = divmod(line * cols, LANES)
            part = parts[at]
            if off:
                part = pltpu.roll(part, LANES - off, 1)
                if off + cols > LANES:
                    part = jnp.where(
                        lane < LANES - off, part, pltpu.roll(parts[at + 1], LANES - off, 1)
                    )
            part = jnp.where(lane < cols, part, 0.0)
            target[half, pl.ds(pl.multiple_of((start + line) * GROUP, GROUP), GROUP), :] = part

    def place_right(source, chunk):
        line = source // col_size * rows
        start = line // cols * LANES + line % cols
        spread(chunk, right_mat, source % col_size, start)

    def place_left(source, chunk):
        spread(chunk, left_mat, source % col_size, source // col_size * rows)

    place_right(flat, right[member])
    place_left(member, left[member])

    def take_right(ahead, step):
        right_copy(ahead, step).wait_recv()
        source = (block - ahead + blocks) % blocks * groups + (member - step + groups) % groups
        place_right(source, right_all[source])

    def take_left(step):
        left_copy(step).wait_recv()
        source = (member - step + groups) % groups
        place_left(source, left_all[source])

    each(1, groups, lambda step: take_right(0, step))
    each(1, groups, take_left)
    block_lines = block_rows * rows

    def channel(target, index, start, count):
        first_line = pl.multiple_of(start * GROUP, GROUP) + index
        return jnp.concatenate(
            [
                target[half, pl.ds(first_line, count, stride=GROUP), :].astype(jnp.bfloat16)
                for half in range(col_size)
            ],
            axis=1,
        )

    for index in range(GROUP):
        left_lines[index] = channel(left_mat, index, 0, block_lines)

    def finish(half):
        for index in range(GROUP):
            made = lax.dot_general(
                left_lines[index],
                channel(right_mat, index, half * LANES, LANES),
                (((1,), (1,)), ((), ())),
                preferred_element_type=jnp.float32,
            )
            product[pl.ds(index, block_lines, stride=GROUP), :] = made

        def pack(step):
            part_row = (member // col_size + step) % block_rows
            to = part_row * col_size + half
            lines = [
                product[pl.ds(pl.multiple_of((part_row * rows + line) * GROUP, GROUP), GROUP), :]
                for line in range(rows)
            ]
            for at in range(pairs // LANES):
                low = at * LANES
                line, off = divmod(low, cols)
                part = pltpu.roll(lines[line], LANES - off, 1) if off else lines[line]
                have = cols - off
                while have < LANES:
                    line += 1
                    part = jnp.where(lane < have, part, pltpu.roll(lines[line], have, 1))
                    have += cols
                triangle[to, :, low : low + LANES] = part.astype(jnp.bfloat16)

            @pl.when(to != member)
            def _():
                back_copy(to, member).start()

        each(0, block_rows, pack)

    finish(block)
    for ahead in range(1, blocks):
        each(0, groups, lambda step: take_right(ahead, step))
        finish((block - ahead + blocks) % blocks)
    owned[member] = triangle[member]
    each(1, groups, lambda step: left_copy(step).wait_send())
    each(1, groups, lambda step: right_copy(0, step).wait_send())
    for ahead in range(1, blocks):
        each(0, groups, lambda step: right_copy(ahead, step).wait_send())

    def wait_back(step):
        other = (member + step) % groups
        back_copy(other, other).wait()

    each(1, groups, wait_back)

    def hand_out(at):
        return pltpu.make_async_copy(
            made_out.at[pl.ds(at, LANES)], out.at[pl.ds(at, LANES)], out_sem.at[at // LANES]
        )

    for at in range(0, pairs, LANES):
        piece = jnp.concatenate(
            [owned[group, :, at : at + LANES].astype(jnp.float32) for group in range(groups)],
            axis=0,
        )
        scaled = norm_axis(piece, 0).T.astype(jnp.bfloat16)
        projected = jnp.dot(scaled, w_out[...], preferred_element_type=jnp.float32)
        made_out[at : at + LANES] = (gate[at : at + LANES] * projected).astype(jnp.bfloat16)
        hand_out(at).start()
    for at in range(0, pairs, LANES):
        hand_out(at).wait()


def fused(sizes, pair_act, tile_mask, *weights):
    row_size, col_size, groups = sizes
    devices = row_size * col_size
    block_rows = groups // col_size
    rows, cols, width = pair_act.shape
    pairs = rows * cols
    kept = pl.BlockSpec(memory_space=pltpu.VMEM)
    dma = pltpu.SemaphoreType.DMA
    chunks = pltpu.VMEM((groups, GROUP, pairs), jnp.bfloat16)
    result = pl.pallas_call(
        functools.partial(fused_kernel, sizes, pair_act.shape),
        out_shape=jax.ShapeDtypeStruct((pairs, width), jnp.bfloat16),
        in_specs=[pl.BlockSpec(memory_space=pltpu.HBM)] * 8,
        out_specs=pl.BlockSpec(memory_space=pltpu.HBM),
        scratch_shapes=[
            pltpu.VMEM((pairs, width), jnp.bfloat16),
            pltpu.VMEM(tile_mask.shape, tile_mask.dtype),
            *[pltpu.VMEM(weight.shape, weight.dtype) for weight in weights],
            dma((8,)),
            pltpu.VMEM((pairs, width), jnp.bfloat16),
            dma((pairs // LANES,)),
            pltpu.VMEM((pairs, width), jnp.bfloat16),
            pltpu.VMEM((pairs, width), jnp.float32),
            chunks,
            chunks,
            chunks,
            pltpu.VMEM((devices, GROUP, pairs), jnp.bfloat16),
            pltpu.VMEM((col_size, block_rows * rows * GROUP, LANES), jnp.float32),
            pltpu.VMEM((col_size, col_size * LANES * GROUP, LANES), jnp.float32),
            pltpu.VMEM((GROUP, block_rows * rows, col_size * LANES), jnp.bfloat16),
            pltpu.VMEM((block_rows * rows * GROUP, LANES), jnp.float32),
            chunks,
            chunks,
            dma((groups,)),
            dma((groups,)),
            dma((devices,)),
            dma((devices,)),
            dma((groups,)),
            dma((groups,)),
        ],
        compiler_params=pltpu.CompilerParams(collective_id=2, has_side_effects=True),
    )(pair_act.reshape(pairs, width), tile_mask, *weights)
    return result.reshape(rows, cols, width)


def fits(sizes, rows, cols):
    row_size, col_size, groups = sizes
    pairs = rows * cols
    if row_size * col_size != groups * col_size or groups % col_size:
        return False
    return cols <= LANES and pairs % LANES == 0 and cols % rows == 0


def solution(mesh):
    def whole(pair_act, tile_mask, *weights):
        groups = pair_act.shape[2] // GROUP
        sizes = (mesh.shape["row"], mesh.shape["col"], groups)
        rows, cols = (pair_act.shape[0] // sizes[0], pair_act.shape[1] // sizes[1])
        body = fused if fits(sizes, rows, cols) else local
        return jax.shard_map(
            functools.partial(body, sizes),
            mesh=mesh,
            in_specs=(P("row", "col", None), P(), P(), P(), P(), P(), P(), P()),
            out_specs=P("row", "col", None),
            check_vma=False,
        )(pair_act, tile_mask, *weights)

    return whole
```

profile of v0, /device:TPU:0, one launch (start us, length us, event | category | flops | bytes accessed | tf_op | source)
XLA Modules:
  0.0 30.0 jit_solution(2457470791879246828)
XLA Ops:
  0.0 28.3 %shard_map.82 = bf16[1152,128]{1,0:T(8,128)(2,1)} custom-call(bf16[1152,128]{1,0:T(8,128)(2,1)} %bitcast.3, s32[12,12]{1,0:T(8,128)} %tiles_in.1, bf16[128,128]{1,0:T(8,128)(2,1)} %rest_0_.1, bf16[128,128]{1,0:T(8,128)(2,1)} %rest_1_.1, bf16[128,128]{1,0:T(8,128)(2,1)} %rest_2_.1, bf16[128,128]{1,0:T(8,128)(2,1)} %rest_3_.1, bf16[128,128]{1,0:T(8,128)(2,1)} %rest_4_.1, ...), custom_call_target="tpu_custom_call" | custom-call | tf_op jit(solution)/shard_map/pallas_call | solution.py:485
  28.3 1.7 %copy.10 = bf16[12,96,128]{2,1,0:T(8,128)(2,1)} copy(bf16[12,96,128]{2,1,0:T(8,128)(2,1)} %bitcast.2) | data formatting | bytes 589824
where the time goes:
time: 30.5 us; the launch traced here: 30 us
  Pallas kernels  28.3 us (93%)
  local copies, waits for them, and re-layouts  1.69 us (6%)
    pallas_call x1, Pallas kernels, fused(): pl.pallas_call(functools.partial(fused_kernel, sizes, pair_act.shape), ou...  28.3 us
    unnamed x1, local copies, waits for them, and re-layouts  1.69 us

commit v1 on v0

--- a/solution.py
+++ b/solution.py
@@ -230,7 +230,7 @@
 ):
     weights_in, out = rest[:6], rest[6]
     (
-        pair, tiles, w_left_gate, w_left, w_right_gate, w_right, w_out_gate, w_out, input_sem, made_out, out_sem,
+        pair, tiles, w_left_gate, w_left, w_right_gate, w_right, w_out_gate, w_out, input_sem,
         normed, gate, left, right, left_all, right_all, left_mat, right_mat, left_lines, product, triangle, owned,
         left_send, left_recv, right_send, right_recv, back_send, back_recv,
     ) = rest[7:]
@@ -455,11 +455,6 @@
 
     each(1, groups, wait_back)
 
-    def hand_out(at):
-        return pltpu.make_async_copy(
-            made_out.at[pl.ds(at, LANES)], out.at[pl.ds(at, LANES)], out_sem.at[at // LANES]
-        )
-
     for at in range(0, pairs, LANES):
         piece = jnp.concatenate(
             [owned[group, :, at : at + LANES].astype(jnp.float32) for group in range(groups)],
@@ -467,10 +462,7 @@
         )
         scaled = norm_axis(piece, 0).T.astype(jnp.bfloat16)
         projected = jnp.dot(scaled, w_out[...], preferred_element_type=jnp.float32)
-        made_out[at : at + LANES] = (gate[at : at + LANES] * projected).astype(jnp.bfloat16)
-        hand_out(at).start()
-    for at in range(0, pairs, LANES):
-        hand_out(at).wait()
+        out[at : at + LANES] = (gate[at : at + LANES] * projected).astype(jnp.bfloat16)
 
 
 def fused(sizes, pair_act, tile_mask, *weights):
@@ -484,16 +476,14 @@
     chunks = pltpu.VMEM((groups, GROUP, pairs), jnp.bfloat16)
     result = pl.pallas_call(
         functools.partial(fused_kernel, sizes, pair_act.shape),
-        out_shape=jax.ShapeDtypeStruct((pairs, width), jnp.bfloat16),
+        out_shape=pltpu.VMEM((pairs, width), jnp.bfloat16),
         in_specs=[pl.BlockSpec(memory_space=pltpu.HBM)] * 8,
-        out_specs=pl.BlockSpec(memory_space=pltpu.HBM),
+        out_specs=pl.BlockSpec(memory_space=pltpu.VMEM),
         scratch_shapes=[
             pltpu.VMEM((pairs, width), jnp.bfloat16),
             pltpu.VMEM(tile_mask.shape, tile_mask.dtype),
             *[pltpu.VMEM(weight.shape, weight.dtype) for weight in weights],
             dma((8,)),
-            pltpu.VMEM((pairs, width), jnp.bfloat16),
-            dma((pairs // LANES,)),
             pltpu.VMEM((pairs, width), jnp.bfloat16),
             pltpu.VMEM((pairs, width), jnp.float32),
             chunks,

time: 30.5 us -> 28.8 us (0.944)
  local copies, waits for them, and re-layouts: 1.69 us -> 0.72 us
  Pallas kernels: 28.3 us -> 27.6 us
    unnamed x1, local copies, waits for them, and re-layouts: 1.69 us -> 0.72 us
    pallas_call x1, Pallas kernels: 28.3 us -> 27.6 us  [fused(): pl.pallas_call(functools.partial(fused_kernel, sizes, pair_act.shape), ou...]
where the time goes in v1:
time: 28.8 us; the launch traced here: 28.3 us
  Pallas kernels  27.6 us (96%)
  local copies, waits for them, and re-layouts  0.72 us (2%)
    pallas_call x1, Pallas kernels, fused(): pl.pallas_call(functools.partial(fused_kernel, sizes, pair_act.shape), ou...  27.6 us
    unnamed x1, local copies, waits for them, and re-layouts  0.72 us

profile of v1, /device:TPU:0, one launch (start us, length us, event | category | flops | bytes accessed | tf_op | source)
XLA Modules:
  0.0 28.3 jit_solution(12305865814846468079)
XLA Ops:
  0.0 27.6 %shard_map.82 = bf16[1152,128]{1,0:T(8,128)(2,1)S(1)} custom-call(bf16[1152,128]{1,0:T(8,128)(2,1)} %bitcast.3, s32[12,12]{1,0:T(8,128)} %tiles_in.1, bf16[128,128]{1,0:T(8,128)(2,1)} %rest_0_.1, bf16[128,128]{1,0:T(8,128)(2,1)} %rest_1_.1, bf16[128,128]{1,0:T(8,128)(2,1)} %rest_2_.1, bf16[128,128]{1,0:T(8,128)(2,1)} %rest_3_.1, bf16[128,128]{1,0:T(8,128)(2,1)} %rest_4_.1, ...), custom_call_target="tpu_custom_call" | custom-call | tf_op jit(solution)/shard_map/pallas_call | solution.py:477
  27.6 0.7 %copy.10 = bf16[12,96,128]{2,1,0:T(8,128)(2,1)} copy(bf16[12,96,128]{2,1,0:T(8,128)(2,1)S(1)} %bitcast.2) | data formatting | bytes 589824

commit v2 on v1

--- a/solution.py
+++ b/solution.py
@@ -223,173 +223,207 @@
 
 
 LANES = 128
-
-
-def fused_kernel(
-    sizes, shape, pair_in, tiles_in, *rest
-):
+QUAD = 4
+
+
+def fused_kernel(sizes, shape, pair_in, tiles_in, *rest):
     weights_in, out = rest[:6], rest[6]
     (
-        pair, tiles, w_left_gate, w_left, w_right_gate, w_right, w_out_gate, w_out, input_sem,
+        pair, tiles, weights, pair_sem, input_sem,
         normed, gate, left, right, left_all, right_all, left_mat, right_mat, left_lines, product, triangle, owned,
-        left_send, left_recv, right_send, right_recv, back_send, back_recv,
+        send, left_recv, right_recv, back_recv,
     ) = rest[7:]
-    kept = (pair, tiles, w_left_gate, w_left, w_right_gate, w_right, w_out_gate, w_out)
-    fetches = [
-        pltpu.make_async_copy(source, target, input_sem.at[index])
-        for index, (source, target) in enumerate(zip((pair_in, tiles_in, *weights_in), kept))
-    ]
     row_size, col_size, groups = sizes
     rows, cols, width = shape
     devices = row_size * col_size
-    blocks = devices // groups
     block_rows = groups // col_size
+    plane_size = groups // 2
     pairs = rows * cols
+    spare = LANES - cols
+    count = pairs // LANES
+    extra = rows - count
+    third = pairs // extra
     tile = rows * row_size // TILES
     row, col = lax.axis_index("row"), lax.axis_index("col")
     flat = row * col_size + col
     member = flat % groups
     block = flat // groups
     first = block * groups
+    plane = flat // plane_size
+    core = flat // col_size % 2
+    moves = [bit * (1 - 2 * (flat // bit % 2)) for bit in (groups, plane_size, QUAD, 1)]
+
+    def reach(flips, to_core):
+        moved = sum(move for flip, move in zip(flips, moves) if flip)
+        return flat + moved + col_size * (to_core - core)
 
     barrier = pltpu.get_barrier_semaphore()
 
-    def signal(step, _):
-        pl.semaphore_signal(
-            barrier, inc=1, device_id=place((flat + step) % devices, col_size), device_id_type=MESH
-        )
-        return 0
-
-    fetches[0].start()
-    lax.fori_loop(1, devices, signal, 0)
-    for fetch in fetches[1:]:
-        fetch.start()
-    fetches[0].wait()
-
-    values = pair[...].astype(jnp.float32)
-    normed[...] = norm_axis(values, 1).astype(jnp.bfloat16)
-
-    for fetch in fetches[1:]:
-        fetch.wait()
-    spot = lax.broadcasted_iota(jnp.int32, (1, pairs), 1)
-    within = spot
-    for line in range(1, rows):
-        within = jnp.where(spot >= line * cols, spot - line * cols, within)
-    tile_ids = lax.broadcasted_iota(jnp.int32, (TILES, pairs), 0)
-    row_low = (tile_ids * tile - row * rows) * cols
-    row_hot = ((spot >= row_low) & (spot < row_low + tile * cols)).astype(jnp.float32)
-    col_low = tile_ids * tile - col * cols
-    col_hot = ((within >= col_low) & (within < col_low + tile)).astype(jnp.float32)
-    picked = jnp.dot(tiles[...].astype(jnp.float32).T, row_hot, preferred_element_type=jnp.float32)
-    mask = jnp.sum(picked * col_hot, axis=0, keepdims=True)
-
-    def project(weight):
-        turned = weight[...].astype(jnp.float32).T.astype(jnp.bfloat16)
+    fetches = [[], []]
+    for part in range(extra):
+        for source, target in (
+            (pair_in.at[part], pair.at[part, :, pl.ds(0, extra)]),
+            (pair_in.at[extra, part], pair.at[part, :, extra]),
+        ):
+            fetches[0].append(pltpu.make_async_copy(source, target, pair_sem.at[part]))
+    for index, source in enumerate(weights_in):
+        fetches[1].append(pltpu.make_async_copy(source, weights.at[index], input_sem.at[0]))
+    tile_fetch = pltpu.make_async_copy(tiles_in, tiles, input_sem.at[1])
+
+    def all_of(ref, sem):
+        return pltpu.make_async_copy(ref, ref, sem)
+
+    with jax.named_scope("a0_begin"):
+        tile_fetch.start()
+        for fetch in fetches[0]:
+            fetch.start()
+
+        def signal(step, _):
+            pl.semaphore_signal(
+                barrier, inc=1, device_id=place((flat + step) % devices, col_size), device_id_type=MESH
+            )
+            return 0
+
+        lax.fori_loop(1, devices, signal, 0)
+        for fetch in fetches[1]:
+            fetch.start()
+        tile_fetch.wait()
+
+    with jax.named_scope("a1_mask"):
+        lane = lax.broadcasted_iota(jnp.int32, (GROUP, LANES), 1)
+        low = lane < cols
+        spot = lax.broadcasted_iota(jnp.int32, (TILES, LANES), 1)
+        tile_low = lax.broadcasted_iota(jnp.int32, (TILES, LANES), 0) * tile
+        direct = spot < cols
+        masks = []
+        turned_tiles = tiles[...].astype(jnp.float32).T
+        for at in range(count):
+            line = row * rows + jnp.where(direct, at, count + at // extra)
+            within = col * cols + jnp.where(direct, spot, spot - cols + at % extra * spare)
+            row_hot = ((line >= tile_low) & (line < tile_low + tile)).astype(jnp.float32)
+            col_hot = ((within >= tile_low) & (within < tile_low + tile)).astype(jnp.float32)
+            picked = jnp.dot(turned_tiles, row_hot, preferred_element_type=jnp.float32)
+            masks.append(jnp.sum(picked * col_hot, axis=0, keepdims=True))
+        mask = jnp.concatenate(masks, axis=1)
+
+    with jax.named_scope("a2_ln"):
+        for part in range(extra):
+            all_of(pair.at[part], pair_sem.at[part]).wait()
+            values = pair[part].reshape(third, width).astype(jnp.float32)
+            normed[part * third : (part + 1) * third] = norm_axis(values, 1).astype(jnp.bfloat16)
+        all_of(weights, input_sem.at[0]).wait()
+
+    def project(index):
+        turned = weights[index].astype(jnp.float32).T.astype(jnp.bfloat16)
         return lax.dot_general(
             turned, normed[...], (((1,), (1,)), ((), ())), preferred_element_type=jnp.float32
         )
 
-    def factor(gate_weight, weight, target):
-        made = jax.nn.sigmoid(project(gate_weight)) * project(weight) * mask
+    def factor(gate_index, index, target):
+        made = jax.nn.sigmoid(project(gate_index)) * project(index) * mask
         for group in range(groups):
             target[group] = made[group * GROUP : (group + 1) * GROUP].astype(jnp.bfloat16)
 
-    def right_copy(ahead, step):
-        to = (member + step) % groups
-        return pltpu.make_async_remote_copy(
-            src_ref=right.at[to],
-            dst_ref=right_all.at[flat],
-            send_sem=right_send.at[ahead * groups + step],
-            recv_sem=right_recv.at[ahead * groups + step],
-            device_id=place((block + ahead) % blocks * groups + to, col_size),
+    def copy_to(source, target, sent, received, to):
+        pltpu.make_async_remote_copy(
+            src_ref=source.at[to % groups],
+            dst_ref=target,
+            send_sem=sent,
+            recv_sem=received,
+            device_id=place(to, col_size),
             device_id_type=MESH,
+        ).start()
+
+    def send_right(to):
+        copy_to(right, right_all.at[flat], send.at[0], right_recv.at[own_quad], to)
+
+    def send_left(to):
+        copy_to(left, left_all.at[member], send.at[1], left_recv.at[member // QUAD], to)
+
+    def keep(source, target, received):
+        return pltpu.make_async_copy(source.at[member], target, received)
+
+    own_quad = flat // QUAD
+    lows = ((1, 1), (0, 1), (1, 0), (0, 0))
+
+    def send_across(to_core):
+        for low_flips in lows:
+            send_right(reach((1, 0, *low_flips), to_core))
+            send_right(reach((1, 1, *low_flips), to_core))
+
+    with jax.named_scope("a3_right"):
+        factor(2, 3, right)
+    with jax.named_scope("a4_bar"):
+        pl.semaphore_wait(barrier, devices - 1)
+    with jax.named_scope("a5_send"):
+        send_across(1)
+    with jax.named_scope("a6_left"):
+        factor(0, 1, left)
+    with jax.named_scope("a7_send"):
+        for low_flips in lows:
+            for to_core in range(2):
+                send_left(reach((0, 1, *low_flips), to_core))
+        for low_flips in lows:
+            send_right(reach((0, 1, *low_flips), 0))
+        for low_flips in lows:
+            send_right(reach((0, 0, *low_flips), 1 - core))
+            send_left(reach((0, 0, *low_flips), 1 - core))
+        for low_flips in lows[:-1]:
+            send_right(reach((0, 0, *low_flips), core))
+            send_left(reach((0, 0, *low_flips), core))
+        send_across(0)
+        for low_flips in lows:
+            send_right(reach((0, 1, *low_flips), 1))
+        keep(left, left_all.at[member], left_recv.at[member // QUAD]).start()
+        keep(right, right_all.at[flat], right_recv.at[own_quad]).start()
+
+    with jax.named_scope("b0_gate"):
+        gate[...] = jax.nn.sigmoid(
+            jnp.dot(normed[...], weights[4], preferred_element_type=jnp.float32)
         )
-
-    def member_copy(source, target, send, recv, step):
-        to = (member + step) % groups
-        return pltpu.make_async_remote_copy(
-            src_ref=source.at[to],
-            dst_ref=target.at[member],
-            send_sem=send.at[step],
-            recv_sem=recv.at[step],
-            device_id=place(first + to, col_size),
-            device_id_type=MESH,
-        )
-
-    def left_copy(step):
-        return member_copy(left, left_all, left_send, left_recv, step)
-
-    def back_copy(to, slot):
-        return pltpu.make_async_remote_copy(
-            src_ref=triangle.at[to],
-            dst_ref=owned.at[slot],
-            send_sem=back_send.at[to],
-            recv_sem=back_recv.at[slot],
-            device_id=place(first + to, col_size),
-            device_id_type=MESH,
-        )
-
-    def each(start, stop, do):
-        def body(step, _):
-            do(step)
-            return 0
-
-        lax.fori_loop(start, stop, body, 0)
-
-    factor(w_right_gate, w_right, right)
-    factor(w_left_gate, w_left, left)
-    pl.semaphore_wait(barrier, devices - 1)
-    each(1, groups, lambda step: right_copy(0, step).start())
-    each(1, groups, lambda step: left_copy(step).start())
-    for ahead in range(1, blocks):
-        each(0, groups, lambda step: right_copy(ahead, step).start())
-
-    gate[...] = jax.nn.sigmoid(
-        jnp.dot(normed[...], w_out_gate[...], preferred_element_type=jnp.float32)
-    )
-    left_mat[...] = jnp.zeros_like(left_mat)
-    right_mat[...] = jnp.zeros_like(right_mat)
-    lane = lax.broadcasted_iota(jnp.int32, (GROUP, LANES), 1)
-
-    def spread(chunk, target, half, start):
+        right_mat[...] = jnp.zeros_like(right_mat)
+
+    def spread(chunk, target, half, start, clean):
         parts = [
             chunk[:, at : at + LANES].astype(jnp.float32) for at in range(0, pairs, LANES)
         ]
-        for line in range(rows):
-            at, off = divmod(line * cols, LANES)
-            part = parts[at]
-            if off:
-                part = pltpu.roll(part, LANES - off, 1)
-                if off + cols > LANES:
-                    part = jnp.where(
-                        lane < LANES - off, part, pltpu.roll(parts[at + 1], LANES - off, 1)
-                    )
-            part = jnp.where(lane < cols, part, 0.0)
-            target[half, pl.ds(pl.multiple_of((start + line) * GROUP, GROUP), GROUP), :] = part
-
-    def place_right(source, chunk):
-        line = source // col_size * rows
-        start = line // cols * LANES + line % cols
-        spread(chunk, right_mat, source % col_size, start)
-
-    def place_left(source, chunk):
-        spread(chunk, left_mat, source % col_size, source // col_size * rows)
-
-    place_right(flat, right[member])
-    place_left(member, left[member])
-
-    def take_right(ahead, step):
-        right_copy(ahead, step).wait_recv()
-        source = (block - ahead + blocks) % blocks * groups + (member - step + groups) % groups
-        place_right(source, right_all[source])
-
-    def take_left(step):
-        left_copy(step).wait_recv()
-        source = (member - step + groups) % groups
-        place_left(source, left_all[source])
-
-    each(1, groups, lambda step: take_right(0, step))
-    each(1, groups, take_left)
+        lines = list(parts)
+        for line in range(extra):
+            base = line * extra
+            made = pltpu.roll(parts[base], spare, 1)
+            for piece in range(1, extra):
+                moved = pltpu.roll(parts[base + piece], (piece + 1) * spare % LANES, 1)
+                made = jnp.where(lane < piece * spare, made, moved)
+            lines.append(made)
+        for line, made in enumerate(lines):
+            if clean:
+                made = jnp.where(low, made, 0.0)
+            target[half, pl.ds(pl.multiple_of((start + line) * GROUP, GROUP), GROUP), :] = made
+
+    def place_right(source):
+        line = source // col_size
+        start = line // block_rows * LANES + line % block_rows * rows
+        spread(right_all[source], right_mat, source % col_size, start, False)
+
+    def place_left(source):
+        spread(left_all[source], left_mat, source % col_size, source // col_size * rows, True)
+
+    def each_of(start, length, do):
+        def body(step, _):
+            for index in range(QUAD):
+                do(start + step * QUAD + index)
+            return 0
+
+        lax.fori_loop(0, length // QUAD, body, 0)
+
+    quads = plane_size // QUAD
+
+    def take(source_all, received, which, put):
+        for step in range(quads):
+            quad = which * quads + step
+            all_of(source_all.at[pl.ds(quad * QUAD, QUAD)], received.at[quad]).wait()
+            each_of(quad * QUAD, QUAD, put)
+
     block_lines = block_rows * rows
 
     def channel(target, index, start, count):
@@ -402,9 +436,6 @@
             axis=1,
         )
 
-    for index in range(GROUP):
-        left_lines[index] = channel(left_mat, index, 0, block_lines)
-
     def finish(half):
         for index in range(GROUP):
             made = lax.dot_general(
@@ -415,54 +446,82 @@
             )
             product[pl.ds(index, block_lines, stride=GROUP), :] = made
 
-        def pack(step):
-            part_row = (member // col_size + step) % block_rows
+        def pack(step, _):
+            part_row = (member // col_size + block_rows // 2 + step) % block_rows
             to = part_row * col_size + half
             lines = [
                 product[pl.ds(pl.multiple_of((part_row * rows + line) * GROUP, GROUP), GROUP), :]
                 for line in range(rows)
             ]
-            for at in range(pairs // LANES):
-                low = at * LANES
-                line, off = divmod(low, cols)
-                part = pltpu.roll(lines[line], LANES - off, 1) if off else lines[line]
-                have = cols - off
-                while have < LANES:
-                    line += 1
-                    part = jnp.where(lane < have, part, pltpu.roll(lines[line], have, 1))
-                    have += cols
-                triangle[to, :, low : low + LANES] = part.astype(jnp.bfloat16)
+            for at in range(count):
+                moved = pltpu.roll(
+                    lines[count + at // extra], (cols - at % extra * spare) % LANES, 1
+                )
+                made = jnp.where(low, lines[at], moved)
+                triangle[to, :, at * LANES : (at + 1) * LANES] = made.astype(jnp.bfloat16)
+
+            @pl.when(to == member)
+            def _():
+                keep(triangle, owned.at[member], back_recv.at[0]).start()
 
             @pl.when(to != member)
             def _():
-                back_copy(to, member).start()
-
-        each(0, block_rows, pack)
-
-    finish(block)
-    for ahead in range(1, blocks):
-        each(0, groups, lambda step: take_right(ahead, step))
-        finish((block - ahead + blocks) % blocks)
-    owned[member] = triangle[member]
-    each(1, groups, lambda step: left_copy(step).wait_send())
-    each(1, groups, lambda step: right_copy(0, step).wait_send())
-    for ahead in range(1, blocks):
-        each(0, groups, lambda step: right_copy(ahead, step).wait_send())
-
-    def wait_back(step):
-        other = (member + step) % groups
-        back_copy(other, other).wait()
-
-    each(1, groups, wait_back)
-
-    for at in range(0, pairs, LANES):
-        piece = jnp.concatenate(
-            [owned[group, :, at : at + LANES].astype(jnp.float32) for group in range(groups)],
-            axis=0,
-        )
-        scaled = norm_axis(piece, 0).T.astype(jnp.bfloat16)
-        projected = jnp.dot(scaled, w_out[...], preferred_element_type=jnp.float32)
-        out[at : at + LANES] = (gate[at : at + LANES] * projected).astype(jnp.bfloat16)
+                pltpu.make_async_remote_copy(
+                    src_ref=triangle.at[to],
+                    dst_ref=owned.at[member],
+                    send_sem=send.at[2],
+                    recv_sem=back_recv.at[0],
+                    device_id=place(first + to, col_size),
+                    device_id_type=MESH,
+                ).start()
+
+            return 0
+
+        lax.fori_loop(0, block_rows, pack, 0)
+
+    early = (block + core) % 2
+    with jax.named_scope("b1_left"):
+        take(left_all, left_recv, plane % 2, place_left)
+    with jax.named_scope("b2_near"):
+        take(right_all, right_recv, early * 2 + plane % 2, place_right)
+    with jax.named_scope("b3_left"):
+        take(left_all, left_recv, 1 - plane % 2, place_left)
+    with jax.named_scope("b4_lines"):
+        for index in range(GROUP):
+            left_lines[index] = channel(left_mat, index, 0, block_lines)
+    with jax.named_scope("b5_far"):
+        take(right_all, right_recv, early * 2 + 1 - plane % 2, place_right)
+    with jax.named_scope("c0_fin"):
+        finish(early)
+    late = 1 - early
+    with jax.named_scope("c1_near"):
+        take(right_all, right_recv, late * 2 + plane % 2, place_right)
+    with jax.named_scope("c2_far"):
+        take(right_all, right_recv, late * 2 + 1 - plane % 2, place_right)
+    with jax.named_scope("c3_fin"):
+        finish(late)
+    with jax.named_scope("d0_back"):
+        all_of(owned, back_recv.at[0]).wait()
+
+    with jax.named_scope("d1_out"):
+        for at in range(count):
+            piece = jnp.concatenate(
+                [
+                    owned[group, :, at * LANES : (at + 1) * LANES].astype(jnp.float32)
+                    for group in range(groups)
+                ],
+                axis=0,
+            )
+            scaled = norm_axis(piece, 0).T.astype(jnp.bfloat16)
+            projected = jnp.dot(scaled, weights[5], preferred_element_type=jnp.float32)
+            made = (gate[at * LANES : (at + 1) * LANES] * projected).astype(jnp.bfloat16)
+            out[at] = made[:cols]
+            start = at % extra * spare
+            out[count + at // extra, start : start + spare] = made[cols:]
+    with jax.named_scope("d2_sent"):
+        all_of(right_all.at[pl.ds(0, devices - 1)], send.at[0]).wait()
+        all_of(left_all.at[pl.ds(0, groups - 1)], send.at[1]).wait()
+        all_of(triangle.at[pl.ds(0, groups - 1)], send.at[2]).wait()
 
 
 def fused(sizes, pair_act, tile_mask, *weights):
@@ -471,19 +530,21 @@
     block_rows = groups // col_size
     rows, cols, width = pair_act.shape
     pairs = rows * cols
-    kept = pl.BlockSpec(memory_space=pltpu.VMEM)
+    spare = LANES - cols
+    extra = rows - pairs // LANES
     dma = pltpu.SemaphoreType.DMA
     chunks = pltpu.VMEM((groups, GROUP, pairs), jnp.bfloat16)
     result = pl.pallas_call(
         functools.partial(fused_kernel, sizes, pair_act.shape),
-        out_shape=pltpu.VMEM((pairs, width), jnp.bfloat16),
+        out_shape=pltpu.VMEM((rows, cols, width), jnp.bfloat16),
         in_specs=[pl.BlockSpec(memory_space=pltpu.HBM)] * 8,
         out_specs=pl.BlockSpec(memory_space=pltpu.VMEM),
         scratch_shapes=[
-            pltpu.VMEM((pairs, width), jnp.bfloat16),
+            pltpu.VMEM((extra, extra, extra + 1, spare, width), jnp.bfloat16),
             pltpu.VMEM(tile_mask.shape, tile_mask.dtype),
-            *[pltpu.VMEM(weight.shape, weight.dtype) for weight in weights],
-            dma((8,)),
+            pltpu.VMEM((6, width, width), jnp.bfloat16),
+            dma((extra,)),
+            dma((2,)),
             pltpu.VMEM((pairs, width), jnp.bfloat16),
             pltpu.VMEM((pairs, width), jnp.float32),
             chunks,
@@ -496,24 +557,26 @@
             pltpu.VMEM((block_rows * rows * GROUP, LANES), jnp.float32),
             chunks,
             chunks,
-            dma((groups,)),
-            dma((groups,)),
-            dma((devices,)),
-            dma((devices,)),
-            dma((groups,)),
-            dma((groups,)),
+            dma((3,)),
+            dma((groups // QUAD,)),
+            dma((devices // QUAD,)),
+            dma((1,)),
         ],
         compiler_params=pltpu.CompilerParams(collective_id=2, has_side_effects=True),
-    )(pair_act.reshape(pairs, width), tile_mask, *weights)
-    return result.reshape(rows, cols, width)
+    )(pair_act.reshape(extra + 1, extra, extra, spare, width), tile_mask, *weights)
+    return result
 
 
 def fits(sizes, rows, cols):
     row_size, col_size, groups = sizes
     pairs = rows * cols
-    if row_size * col_size != groups * col_size or groups % col_size:
+    spare = LANES - cols
+    extra = rows - pairs // LANES
+    if (row_size, col_size, groups) != (16, 2, 16):
         return False
-    return cols <= LANES and pairs % LANES == 0 and cols % rows == 0
+    if spare <= 0 or pairs % LANES or extra <= 0:
+        return False
+    return rows == extra * (extra + 1) and cols == extra * spare
 
 
 def solution(mesh):

time: 28.8 us -> 27.7 us (0.962); the launches traced: 28.3 us -> 27.5 us
  Pallas kernels: 27.6 us -> 26.8 us
    pallas_call x1, Pallas kernels: 27.6 us -> 26.8 us  [fused(): pl.pallas_call(functools.partial(fused_kernel, sizes, pair_act.shape), ou...]
where the time goes in v2:
time: 27.7 us; the launch traced here: 27.5 us
  Pallas kernels  26.8 us (97%)
  local copies, waits for them, and re-layouts  0.72 us (3%)
    pallas_call x1, Pallas kernels, fused(): pl.pallas_call(functools.partial(fused_kernel, sizes, pair_act.shape), ou...  26.8 us
    unnamed x1, local copies, waits for them, and re-layouts  0.72 us

profile of v2, /device:TPU:0, one launch (start us, length us, event | category | flops | bytes accessed | tf_op | source)
XLA Modules:
  0.0 27.5 jit_solution(13070431818499064293)
XLA Ops:
  0.0 26.8 %shard_map.82 = bf16[12,96,128]{2,1,0:T(8,128)(2,1)S(1)} custom-call(bf16[4,3,3,32,128]{4,3,2,1,0:T(8,128)(2,1)} %bitcast.1, s32[12,12]{1,0:T(8,128)} %tiles_in.1, bf16[128,128]{1,0:T(8,128)(2,1)} %rest_0_.1, bf16[128,128]{1,0:T(8,128)(2,1)} %rest_1_.1, bf16[128,128]{1,0:T(8,128)(2,1)} %rest_2_.1, bf16[128,128]{1,0:T(8,128)(2,1)} %rest_3_.1, ...), custom_call_target="tpu_custom_call" | custom-call | tf_op jit(solution)/shard_map/pallas_call | solution.py:537
  26.8 0.7 %copy.10 = bf16[12,96,128]{2,1,0:T(8,128)(2,1)} copy(bf16[12,96,128]{2,1,0:T(8,128)(2,1)S(1)} %shard_map.82) | data formatting | bytes 589824

commit v3 on v2

--- a/solution.py
+++ b/solution.py
@@ -346,17 +346,23 @@
     own_quad = flat // QUAD
     lows = ((1, 1), (0, 1), (1, 0), (0, 0))
 
-    def send_across(to_core):
+    inner_flip = (plane % 2 + block) % 2
+    to_inner = inner_flip * moves[1]
+    to_outer = (1 - inner_flip) * moves[1]
+
+    def send_across(to_core, shift):
         for low_flips in lows:
-            send_right(reach((1, 0, *low_flips), to_core))
-            send_right(reach((1, 1, *low_flips), to_core))
+            send_right(reach((1, 0, *low_flips), to_core) + shift)
 
     with jax.named_scope("a3_right"):
         factor(2, 3, right)
     with jax.named_scope("a4_bar"):
         pl.semaphore_wait(barrier, devices - 1)
     with jax.named_scope("a5_send"):
-        send_across(1)
+        for low_flips in lows:
+            send_right(reach((1, 0, *low_flips), 0))
+            send_right(reach((0, 1, *low_flips), 1))
+            send_right(reach((1, 1, *low_flips), 0))
     with jax.named_scope("a6_left"):
         factor(0, 1, left)
     with jax.named_scope("a7_send"):
@@ -364,24 +370,27 @@
             for to_core in range(2):
                 send_left(reach((0, 1, *low_flips), to_core))
         for low_flips in lows:
-            send_right(reach((0, 1, *low_flips), 0))
-        for low_flips in lows:
             send_right(reach((0, 0, *low_flips), 1 - core))
             send_left(reach((0, 0, *low_flips), 1 - core))
         for low_flips in lows[:-1]:
             send_right(reach((0, 0, *low_flips), core))
             send_left(reach((0, 0, *low_flips), core))
-        send_across(0)
         for low_flips in lows:
-            send_right(reach((0, 1, *low_flips), 1))
+            send_right(reach((0, 1, *low_flips), 0))
+        send_across(1, to_inner)
+        send_across(1, to_outer)
         keep(left, left_all.at[member], left_recv.at[member // QUAD]).start()
         keep(right, right_all.at[flat], right_recv.at[own_quad]).start()
 
     with jax.named_scope("b0_gate"):
-        gate[...] = jax.nn.sigmoid(
+        opened = jax.nn.sigmoid(
             jnp.dot(normed[...], weights[4], preferred_element_type=jnp.float32)
         )
-        right_mat[...] = jnp.zeros_like(right_mat)
+        for at in range(count):
+            middle = at * LANES + cols
+            start = at % extra * spare
+            gate[at] = opened[at * LANES : middle]
+            gate[count + at // extra, start : start + spare] = opened[middle : middle + spare]
 
     def spread(chunk, target, half, start, clean):
         parts = [
@@ -401,9 +410,7 @@
             target[half, pl.ds(pl.multiple_of((start + line) * GROUP, GROUP), GROUP), :] = made
 
     def place_right(source):
-        line = source // col_size
-        start = line // block_rows * LANES + line % block_rows * rows
-        spread(right_all[source], right_mat, source % col_size, start, False)
+        spread(right_all[source], right_mat, source % col_size, source // col_size * rows, False)
 
     def place_left(source):
         spread(left_all[source], left_mat, source % col_size, source // col_size * rows, True)
@@ -436,50 +443,72 @@
             axis=1,
         )
 
-    def finish(half):
+    part = cols // 2
+    tiles_back = rows // 2 - 1
+
+    def finish(which):
+        half, side = which // 2, which % 2
         for index in range(GROUP):
+            held = channel(right_mat, index, which * part, part)
             made = lax.dot_general(
                 left_lines[index],
-                channel(right_mat, index, half * LANES, LANES),
+                jnp.concatenate([held, held, held[:spare]], axis=0),
                 (((1,), (1,)), ((), ())),
                 preferred_element_type=jnp.float32,
             )
             product[pl.ds(index, block_lines, stride=GROUP), :] = made
 
-        def pack(step, _):
-            part_row = (member // col_size + block_rows // 2 + step) % block_rows
+        def pack(part_row):
             to = part_row * col_size + half
             lines = [
                 product[pl.ds(pl.multiple_of((part_row * rows + line) * GROUP, GROUP), GROUP), :]
                 for line in range(rows)
             ]
-            for at in range(count):
-                moved = pltpu.roll(
-                    lines[count + at // extra], (cols - at % extra * spare) % LANES, 1
+            one, two = lines[rows - 2], lines[rows - 1]
+            ends = [one, two]
+            ends.append(
+                jnp.where(
+                    lane < LANES - spare // 2,
+                    pltpu.roll(one, cols - spare, 1),
+                    pltpu.roll(two, LANES - spare // 2 - part - spare, 1),
                 )
-                made = jnp.where(low, lines[at], moved)
-                triangle[to, :, at * LANES : (at + 1) * LANES] = made.astype(jnp.bfloat16)
+            )
+            for at in range(tiles_back):
+                made = jnp.where(lane < part, lines[2 * at], lines[2 * at + 1])
+                if at < len(ends):
+                    made = jnp.where(low, made, ends[at])
+                triangle[to, side, :, at * LANES : (at + 1) * LANES] = made.astype(jnp.bfloat16)
+
+        def give(part_row):
+            to = part_row * col_size + half
 
             @pl.when(to == member)
             def _():
-                keep(triangle, owned.at[member], back_recv.at[0]).start()
+                pltpu.make_async_copy(
+                    triangle.at[to, side], owned.at[member, side], back_recv.at[0]
+                ).start()
 
             @pl.when(to != member)
             def _():
                 pltpu.make_async_remote_copy(
-                    src_ref=triangle.at[to],
-                    dst_ref=owned.at[member],
+                    src_ref=triangle.at[to, side],
+                    dst_ref=owned.at[member, side],
                     send_sem=send.at[2],
                     recv_sem=back_recv.at[0],
                     device_id=place(first + to, col_size),
                     device_id_type=MESH,
                 ).start()
 
+        def packs(step, _):
+            for index in range(QUAD):
+                pack(step * QUAD + index)
+            for index in range(QUAD):
+                give(step * QUAD + index)
             return 0
 
-        lax.fori_loop(0, block_rows, pack, 0)
-
-    early = (block + core) % 2
+        lax.fori_loop(0, block_rows // QUAD, packs, 0)
+
+    early = (block + 1 - core) % 2
     with jax.named_scope("b1_left"):
         take(left_all, left_recv, plane % 2, place_left)
     with jax.named_scope("b2_near"):
@@ -489,35 +518,47 @@
     with jax.named_scope("b4_lines"):
         for index in range(GROUP):
             left_lines[index] = channel(left_mat, index, 0, block_lines)
+    with jax.named_scope("c0_fin"):
+        finish(early * 2 + plane % 2)
     with jax.named_scope("b5_far"):
         take(right_all, right_recv, early * 2 + 1 - plane % 2, place_right)
-    with jax.named_scope("c0_fin"):
-        finish(early)
+    with jax.named_scope("c1_fin"):
+        finish(early * 2 + 1 - plane % 2)
     late = 1 - early
-    with jax.named_scope("c1_near"):
+    with jax.named_scope("c2_near"):
         take(right_all, right_recv, late * 2 + plane % 2, place_right)
-    with jax.named_scope("c2_far"):
+    with jax.named_scope("c3_fin"):
+        finish(late * 2 + plane % 2)
+    with jax.named_scope("c4_far"):
         take(right_all, right_recv, late * 2 + 1 - plane % 2, place_right)
-    with jax.named_scope("c3_fin"):
-        finish(late)
+    with jax.named_scope("c5_fin"):
+        finish(late * 2 + 1 - plane % 2)
     with jax.named_scope("d0_back"):
         all_of(owned, back_recv.at[0]).wait()
 
     with jax.named_scope("d1_out"):
-        for at in range(count):
+        for side, at in [(side, at) for side in range(2) for at in range(tiles_back)]:
             piece = jnp.concatenate(
                 [
-                    owned[group, :, at * LANES : (at + 1) * LANES].astype(jnp.float32)
+                    owned[group, side, :, at * LANES : (at + 1) * LANES].astype(jnp.float32)
                     for group in range(groups)
                 ],
                 axis=0,
             )
             scaled = norm_axis(piece, 0).T.astype(jnp.bfloat16)
             projected = jnp.dot(scaled, weights[5], preferred_element_type=jnp.float32)
-            made = (gate[at * LANES : (at + 1) * LANES] * projected).astype(jnp.bfloat16)
-            out[at] = made[:cols]
-            start = at % extra * spare
-            out[count + at // extra, start : start + spare] = made[cols:]
+            base = side * part
+            spots = [(2 * at, base, 0, part), (2 * at + 1, base, part, part)]
+            if at < 2:
+                spots.append((rows - 2 + at, base, cols, spare))
+            if at == 2:
+                rest = part - spare
+                spots.append((rows - 2, base + spare, cols, rest))
+                spots.append((rows - 1, base + spare, cols + rest, rest))
+            for line, start, begin, length in spots:
+                stop = start + length
+                made = gate[line, start:stop] * projected[begin : begin + length]
+                out[line, start:stop] = made.astype(jnp.bfloat16)
     with jax.named_scope("d2_sent"):
         all_of(right_all.at[pl.ds(0, devices - 1)], send.at[0]).wait()
         all_of(left_all.at[pl.ds(0, groups - 1)], send.at[1]).wait()
@@ -534,6 +575,7 @@
     extra = rows - pairs // LANES
     dma = pltpu.SemaphoreType.DMA
     chunks = pltpu.VMEM((groups, GROUP, pairs), jnp.bfloat16)
+    parts = pltpu.VMEM((groups, 2, GROUP, (rows // 2 - 1) * LANES), jnp.bfloat16)
     result = pl.pallas_call(
         functools.partial(fused_kernel, sizes, pair_act.shape),
         out_shape=pltpu.VMEM((rows, cols, width), jnp.bfloat16),
@@ -546,17 +588,17 @@
             dma((extra,)),
             dma((2,)),
             pltpu.VMEM((pairs, width), jnp.bfloat16),
-            pltpu.VMEM((pairs, width), jnp.float32),
+            pltpu.VMEM((rows, cols, width), jnp.float32),
             chunks,
             chunks,
             chunks,
             pltpu.VMEM((devices, GROUP, pairs), jnp.bfloat16),
             pltpu.VMEM((col_size, block_rows * rows * GROUP, LANES), jnp.float32),
-            pltpu.VMEM((col_size, col_size * LANES * GROUP, LANES), jnp.float32),
+            pltpu.VMEM((col_size, row_size * rows * GROUP, LANES), jnp.float32),
             pltpu.VMEM((GROUP, block_rows * rows, col_size * LANES), jnp.bfloat16),
             pltpu.VMEM((block_rows * rows * GROUP, LANES), jnp.float32),
-            chunks,
-            chunks,
+            parts,
+            parts,
             dma((3,)),
             dma((groups // QUAD,)),
             dma((devices // QUAD,)),
@@ -575,6 +617,9 @@
     if (row_size, col_size, groups) != (16, 2, 16):
         return False
     if spare <= 0 or pairs % LANES or extra <= 0:
+        return False
+    part = cols // 2
+    if 2 * part != cols or 2 * (part - spare) != spare or rows % 2:
         return False
     return rows == extra * (extra + 1) and cols == extra * spare
 

time: 27.7 us -> 26.3 us (0.949)
  Pallas kernels: 26.8 us -> 25.4 us
    pallas_call x1, Pallas kernels: 26.8 us -> 25.4 us  [fused(): pl.pallas_call(functools.partial(fused_kernel, sizes, pair_act.shape), ou...]
where the time goes in v3:
time: 26.3 us; the launch traced here: 26.2 us
  Pallas kernels  25.4 us (97%)
  local copies, waits for them, and re-layouts  0.72 us (3%)
    pallas_call x1, Pallas kernels, fused(): pl.pallas_call(functools.partial(fused_kernel, sizes, pair_act.shape), ou...  25.4 us
    unnamed x1, local copies, waits for them, and re-layouts  0.72 us

profile of v3, /device:TPU:0, one launch (start us, length us, event | category | flops | bytes accessed | tf_op | source)
XLA Modules:
  0.0 26.2 jit_solution(9920407752642187460)
XLA Ops:
  0.0 25.4 %shard_map.82 = bf16[12,96,128]{2,1,0:T(8,128)(2,1)S(1)} custom-call(bf16[4,3,3,32,128]{4,3,2,1,0:T(8,128)(2,1)} %bitcast.1, s32[12,12]{1,0:T(8,128)} %tiles_in.1, bf16[128,128]{1,0:T(8,128)(2,1)} %rest_0_.1, bf16[128,128]{1,0:T(8,128)(2,1)} %rest_1_.1, bf16[128,128]{1,0:T(8,128)(2,1)} %rest_2_.1, bf16[128,128]{1,0:T(8,128)(2,1)} %rest_3_.1, ...), custom_call_target="tpu_custom_call" | custom-call | tf_op jit(solution)/shard_map/pallas_call | solution.py:579
  25.4 0.7 %copy.10 = bf16[12,96,128]{2,1,0:T(8,128)(2,1)} copy(bf16[12,96,128]{2,1,0:T(8,128)(2,1)S(1)} %shard_map.82) | data formatting | bytes 589824

commit v4 on v3

--- a/solution.py
+++ b/solution.py
@@ -231,7 +231,7 @@
     (
         pair, tiles, weights, pair_sem, input_sem,
         normed, gate, left, right, left_all, right_all, left_mat, right_mat, left_lines, product, triangle, owned,
-        send, left_recv, right_recv, back_recv,
+        send, left_recv, right_recv, back_recv, heard,
     ) = rest[7:]
     row_size, col_size, groups = sizes
     rows, cols, width = shape
@@ -258,6 +258,12 @@
         return flat + moved + col_size * (to_core - core)
 
     barrier = pltpu.get_barrier_semaphore()
+    sides = ((1, 0), (0, 1))
+
+    def tell(semaphore, to):
+        pl.semaphore_signal(
+            semaphore, inc=1, device_id=place(to, col_size), device_id_type=MESH
+        )
 
     fetches = [[], []]
     for part in range(extra):
@@ -278,13 +284,12 @@
         for fetch in fetches[0]:
             fetch.start()
 
-        def signal(step, _):
-            pl.semaphore_signal(
-                barrier, inc=1, device_id=place((flat + step) % devices, col_size), device_id_type=MESH
-            )
-            return 0
-
-        lax.fori_loop(1, devices, signal, 0)
+        for flips in sides:
+            tell(barrier, reach((0, 0, *flips), core))
+        for flips in ((1, 1), (1, 0), (0, 1)):
+            for to_core in range(2):
+                tell(barrier, reach((*flips, 0, 0), to_core))
+        tell(barrier, reach((0, 0, 0, 0), 1 - core))
         for fetch in fetches[1]:
             fetch.start()
         tile_fetch.wait()
@@ -345,40 +350,72 @@
 
     own_quad = flat // QUAD
     lows = ((1, 1), (0, 1), (1, 0), (0, 0))
-
     inner_flip = (plane % 2 + block) % 2
     to_inner = inner_flip * moves[1]
     to_outer = (1 - inner_flip) * moves[1]
 
-    def send_across(to_core, shift):
-        for low_flips in lows:
-            send_right(reach((1, 0, *low_flips), to_core) + shift)
+    outer = (plane // 2 + plane + 1) % 2
+
+    def send_across(low_flips, to_core, shift):
+        send_right(reach((1, 0, *low_flips), to_core) + shift)
+
+    def send_beside(low_flips, to_core):
+        send_right(reach((0, 1, *low_flips), to_core))
+
+    def send_early(low_flips):
+        send_across(low_flips, 0, to_outer)
+        send_beside(low_flips, 1)
+
+        @pl.when(outer == 1)
+        def _():
+            send_beside(low_flips, 0)
+
+    def send_lefts(low_flips):
+        for to_core in range(2):
+            send_left(reach((0, 1, *low_flips), to_core))
 
     with jax.named_scope("a3_right"):
         factor(2, 3, right)
     with jax.named_scope("a4_bar"):
-        pl.semaphore_wait(barrier, devices - 1)
+        pl.semaphore_wait(barrier, 9)
+        for index, flips in enumerate(sides):
+            tell(heard.at[index], reach((0, 0, *flips), core))
     with jax.named_scope("a5_send"):
-        for low_flips in lows:
-            send_right(reach((1, 0, *low_flips), 0))
-            send_right(reach((0, 1, *low_flips), 1))
-            send_right(reach((1, 1, *low_flips), 0))
+        send_early(lows[3])
     with jax.named_scope("a6_left"):
         factor(0, 1, left)
     with jax.named_scope("a7_send"):
-        for low_flips in lows:
-            for to_core in range(2):
-                send_left(reach((0, 1, *low_flips), to_core))
+        send_lefts(lows[3])
+    with jax.named_scope("a8_hear"):
+        pl.semaphore_wait(heard.at[0], 1)
+        tell(heard.at[2], reach((0, 0, *sides[1]), core))
+        pl.semaphore_wait(heard.at[1], 1)
+    with jax.named_scope("a9_send"):
+        for low_flips in lows[1:3]:
+            send_early(low_flips)
+            send_lefts(low_flips)
+    with jax.named_scope("a91_hear"):
+        pl.semaphore_wait(heard.at[2], 1)
+    with jax.named_scope("a92_send"):
+        send_early(lows[0])
+        send_lefts(lows[0])
         for low_flips in lows:
             send_right(reach((0, 0, *low_flips), 1 - core))
             send_left(reach((0, 0, *low_flips), 1 - core))
         for low_flips in lows[:-1]:
             send_right(reach((0, 0, *low_flips), core))
             send_left(reach((0, 0, *low_flips), core))
+
+        @pl.when(outer == 0)
+        def _():
+            for low_flips in lows:
+                send_beside(low_flips, 0)
+
         for low_flips in lows:
-            send_right(reach((0, 1, *low_flips), 0))
-        send_across(1, to_inner)
-        send_across(1, to_outer)
+            send_across(low_flips, 1, to_outer)
+        for low_flips in lows:
+            send_across(low_flips, 0, to_inner)
+            send_across(low_flips, 1, to_inner)
         keep(left, left_all.at[member], left_recv.at[member // QUAD]).start()
         keep(right, right_all.at[flat], right_recv.at[own_quad]).start()
 
@@ -508,7 +545,7 @@
 
         lax.fori_loop(0, block_rows // QUAD, packs, 0)
 
-    early = (block + 1 - core) % 2
+    early = (block + outer * (1 - core)) % 2
     with jax.named_scope("b1_left"):
         take(left_all, left_recv, plane % 2, place_left)
     with jax.named_scope("b2_near"):
@@ -603,6 +640,7 @@
             dma((groups // QUAD,)),
             dma((devices // QUAD,)),
             dma((1,)),
+            pltpu.SemaphoreType.REGULAR((3,)),
         ],
         compiler_params=pltpu.CompilerParams(collective_id=2, has_side_effects=True),
     )(pair_act.reshape(extra + 1, extra, extra, spare, width), tile_mask, *weights)

time: 26.3 us -> 25.8 us (0.981)
  Pallas kernels: 25.4 us -> 25 us
    pallas_call x1, Pallas kernels: 25.4 us -> 25 us  [fused(): pl.pallas_call(functools.partial(fused_kernel, sizes, pair_act.shape), ou...]
where the time goes in v4:
time: 25.8 us; the launch traced here: 25.7 us
  Pallas kernels  25 us (97%)
  local copies, waits for them, and re-layouts  0.72 us (3%)
    pallas_call x1, Pallas kernels, fused(): pl.pallas_call(functools.partial(fused_kernel, sizes, pair_act.shape), ou...  25 us
    unnamed x1, local copies, waits for them, and re-layouts  0.72 us

profile of v4, /device:TPU:0, one launch (start us, length us, event | category | flops | bytes accessed | tf_op | source)
XLA Modules:
  0.0 25.7 jit_solution(3884888882139096554)
XLA Ops:
  0.0 25.0 %shard_map.82 = bf16[12,96,128]{2,1,0:T(8,128)(2,1)S(1)} custom-call(bf16[4,3,3,32,128]{4,3,2,1,0:T(8,128)(2,1)} %bitcast.1, s32[12,12]{1,0:T(8,128)} %tiles_in.1, bf16[128,128]{1,0:T(8,128)(2,1)} %rest_0_.1, bf16[128,128]{1,0:T(8,128)(2,1)} %rest_1_.1, bf16[128,128]{1,0:T(8,128)(2,1)} %rest_2_.1, bf16[128,128]{1,0:T(8,128)(2,1)} %rest_3_.1, ...), custom_call_target="tpu_custom_call" | custom-call | tf_op jit(solution)/shard_map/pallas_call | solution.py:616
  25.0 0.7 %copy.10 = bf16[12,96,128]{2,1,0:T(8,128)(2,1)} copy(bf16[12,96,128]{2,1,0:T(8,128)(2,1)S(1)} %shard_map.82) | data formatting | bytes 589824

commit v5 on v4

--- a/solution.py
+++ b/solution.py
@@ -242,7 +242,6 @@
     spare = LANES - cols
     count = pairs // LANES
     extra = rows - count
-    third = pairs // extra
     tile = rows * row_size // TILES
     row, col = lax.axis_index("row"), lax.axis_index("col")
     flat = row * col_size + col
@@ -271,7 +270,7 @@
             (pair_in.at[part], pair.at[part, :, pl.ds(0, extra)]),
             (pair_in.at[extra, part], pair.at[part, :, extra]),
         ):
-            fetches[0].append(pltpu.make_async_copy(source, target, pair_sem.at[part]))
+            fetches[0].append(pltpu.make_async_copy(source, target, pair_sem.at[0]))
     for index, source in enumerate(weights_in):
         fetches[1].append(pltpu.make_async_copy(source, weights.at[index], input_sem.at[0]))
     tile_fetch = pltpu.make_async_copy(tiles_in, tiles, input_sem.at[1])
@@ -293,6 +292,7 @@
         for fetch in fetches[1]:
             fetch.start()
         tile_fetch.wait()
+        all_of(pair, pair_sem.at[0]).wait()
 
     with jax.named_scope("a1_mask"):
         lane = lax.broadcasted_iota(jnp.int32, (GROUP, LANES), 1)
@@ -312,10 +312,8 @@
         mask = jnp.concatenate(masks, axis=1)
 
     with jax.named_scope("a2_ln"):
-        for part in range(extra):
-            all_of(pair.at[part], pair_sem.at[part]).wait()
-            values = pair[part].reshape(third, width).astype(jnp.float32)
-            normed[part * third : (part + 1) * third] = norm_axis(values, 1).astype(jnp.bfloat16)
+        values = pair[...].reshape(pairs, width).astype(jnp.float32)
+        normed[...] = norm_axis(values, 1).astype(jnp.bfloat16)
         all_of(weights, input_sem.at[0]).wait()
 
     def project(index):
@@ -363,12 +361,12 @@
         send_right(reach((0, 1, *low_flips), to_core))
 
     def send_early(low_flips):
+        send_across(low_flips, 1, to_inner)
         send_across(low_flips, 0, to_outer)
+
+    def send_besides(low_flips):
+        send_beside(low_flips, 0)
         send_beside(low_flips, 1)
-
-        @pl.when(outer == 1)
-        def _():
-            send_beside(low_flips, 0)
 
     def send_lefts(low_flips):
         for to_core in range(2):
@@ -381,24 +379,58 @@
         for index, flips in enumerate(sides):
             tell(heard.at[index], reach((0, 0, *flips), core))
     with jax.named_scope("a5_send"):
-        send_early(lows[3])
+
+        @pl.when(outer == 1)
+        def _():
+            send_besides(lows[3])
+
+        @pl.when(outer == 0)
+        def _():
+            send_early(lows[3])
+
     with jax.named_scope("a6_left"):
         factor(0, 1, left)
     with jax.named_scope("a7_send"):
         send_lefts(lows[3])
-    with jax.named_scope("a8_hear"):
-        pl.semaphore_wait(heard.at[0], 1)
-        tell(heard.at[2], reach((0, 0, *sides[1]), core))
-        pl.semaphore_wait(heard.at[1], 1)
-    with jax.named_scope("a9_send"):
-        for low_flips in lows[1:3]:
+
+        @pl.when(outer == 1)
+        def _():
+            send_early(lows[3])
+
+    def send_mixed(low_flips):
+        @pl.when(outer == 1)
+        def _():
+            send_lefts(low_flips)
+            send_besides(low_flips)
+            send_early(low_flips)
+
+        @pl.when(outer == 0)
+        def _():
             send_early(low_flips)
             send_lefts(low_flips)
+
+    def hear(index):
+        pl.semaphore_wait(heard.at[index], 1)
+        if index == 0:
+            tell(heard.at[2], reach((0, 0, *sides[1]), core))
+        send_mixed(sides[index])
+
+    with jax.named_scope("a8_hear"):
+
+        @pl.when(col == 0)
+        def _():
+            hear(0)
+            hear(1)
+
+        @pl.when(col != 0)
+        def _():
+            hear(1)
+            hear(0)
+
     with jax.named_scope("a91_hear"):
         pl.semaphore_wait(heard.at[2], 1)
     with jax.named_scope("a92_send"):
-        send_early(lows[0])
-        send_lefts(lows[0])
+        send_mixed(lows[0])
         for low_flips in lows:
             send_right(reach((0, 0, *low_flips), 1 - core))
             send_left(reach((0, 0, *low_flips), 1 - core))
@@ -410,12 +442,12 @@
         def _():
             for low_flips in lows:
                 send_beside(low_flips, 0)
-
-        for low_flips in lows:
-            send_across(low_flips, 1, to_outer)
+            for low_flips in lows:
+                send_beside(low_flips, 1)
+
         for low_flips in lows:
             send_across(low_flips, 0, to_inner)
-            send_across(low_flips, 1, to_inner)
+            send_across(low_flips, 1, to_outer)
         keep(left, left_all.at[member], left_recv.at[member // QUAD]).start()
         keep(right, right_all.at[flat], right_recv.at[own_quad]).start()
 
@@ -545,7 +577,7 @@
 
         lax.fori_loop(0, block_rows // QUAD, packs, 0)
 
-    early = (block + outer * (1 - core)) % 2
+    early = block
     with jax.named_scope("b1_left"):
         take(left_all, left_recv, plane % 2, place_left)
     with jax.named_scope("b2_near"):
@@ -561,15 +593,14 @@
         take(right_all, right_recv, early * 2 + 1 - plane % 2, place_right)
     with jax.named_scope("c1_fin"):
         finish(early * 2 + 1 - plane % 2)
-    late = 1 - early
     with jax.named_scope("c2_near"):
-        take(right_all, right_recv, late * 2 + plane % 2, place_right)
+        take(right_all, right_recv, 2 - block, place_right)
     with jax.named_scope("c3_fin"):
-        finish(late * 2 + plane % 2)
+        finish(2 - block)
     with jax.named_scope("c4_far"):
-        take(right_all, right_recv, late * 2 + 1 - plane % 2, place_right)
+        take(right_all, right_recv, 3 - 3 * block, place_right)
     with jax.named_scope("c5_fin"):
-        finish(late * 2 + 1 - plane % 2)
+        finish(3 - 3 * block)
     with jax.named_scope("d0_back"):
         all_of(owned, back_recv.at[0]).wait()
 
@@ -622,7 +653,7 @@
             pltpu.VMEM((extra, extra, extra + 1, spare, width), jnp.bfloat16),
             pltpu.VMEM(tile_mask.shape, tile_mask.dtype),
             pltpu.VMEM((6, width, width), jnp.bfloat16),
-            dma((extra,)),
+            dma((1,)),
             dma((2,)),
             pltpu.VMEM((pairs, width), jnp.bfloat16),
             pltpu.VMEM((rows, cols, width), jnp.float32),

time: 25.8 us -> 25.4 us (0.984)
  Pallas kernels: 25 us -> 24.5 us
    pallas_call x1, Pallas kernels: 25 us -> 24.5 us  [fused(): pl.pallas_call(functools.partial(fused_kernel, sizes, pair_act.shape), ou...]
where the time goes in v5:
time: 25.4 us; the launch traced here: 25.2 us
  Pallas kernels  24.5 us (96%)
  local copies, waits for them, and re-layouts  0.72 us (3%)
    pallas_call x1, Pallas kernels, fused(): pl.pallas_call(functools.partial(fused_kernel, sizes, pair_act.shape), ou...  24.5 us
    unnamed x1, local copies, waits for them, and re-layouts  0.72 us

profile of v5, /device:TPU:0, one launch (start us, length us, event | category | flops | bytes accessed | tf_op | source)
XLA Modules:
  0.0 25.2 jit_solution(5127478825465651799)
XLA Ops:
  0.0 24.5 %shard_map.82 = bf16[12,96,128]{2,1,0:T(8,128)(2,1)S(1)} custom-call(bf16[4,3,3,32,128]{4,3,2,1,0:T(8,128)(2,1)} %bitcast.1, s32[12,12]{1,0:T(8,128)} %tiles_in.1, bf16[128,128]{1,0:T(8,128)(2,1)} %rest_0_.1, bf16[128,128]{1,0:T(8,128)(2,1)} %rest_1_.1, bf16[128,128]{1,0:T(8,128)(2,1)} %rest_2_.1, bf16[128,128]{1,0:T(8,128)(2,1)} %rest_3_.1, ...), custom_call_target="tpu_custom_call" | custom-call | tf_op jit(solution)/shard_map/pallas_call | solution.py:647
  24.5 0.7 %copy.10 = bf16[12,96,128]{2,1,0:T(8,128)(2,1)} copy(bf16[12,96,128]{2,1,0:T(8,128)(2,1)S(1)} %shard_map.82) | data formatting | bytes 589824

commit v6 on v5

--- a/solution.py
+++ b/solution.py
@@ -397,6 +397,10 @@
         def _():
             send_early(lows[3])
 
+    def send_level(low_flips, to_core):
+        send_right(reach((0, 0, *low_flips), to_core))
+        send_left(reach((0, 0, *low_flips), to_core))
+
     def send_mixed(low_flips):
         @pl.when(outer == 1)
         def _():
@@ -409,6 +413,9 @@
             send_early(low_flips)
             send_lefts(low_flips)
 
+        send_level(low_flips, 0)
+        send_level(low_flips, 1)
+
     def hear(index):
         pl.semaphore_wait(heard.at[index], 1)
         if index == 0:
@@ -416,6 +423,7 @@
         send_mixed(sides[index])
 
     with jax.named_scope("a8_hear"):
+        send_level(lows[3], 1 - core)
 
         @pl.when(col == 0)
         def _():
@@ -431,12 +439,6 @@
         pl.semaphore_wait(heard.at[2], 1)
     with jax.named_scope("a92_send"):
         send_mixed(lows[0])
-        for low_flips in lows:
-            send_right(reach((0, 0, *low_flips), 1 - core))
-            send_left(reach((0, 0, *low_flips), 1 - core))
-        for low_flips in lows[:-1]:
-            send_right(reach((0, 0, *low_flips), core))
-            send_left(reach((0, 0, *low_flips), core))
 
         @pl.when(outer == 0)
         def _():
@@ -577,30 +579,27 @@
 
         lax.fori_loop(0, block_rows // QUAD, packs, 0)
 
-    early = block
+    across_inner, across_outer = 2 - block, 3 - 3 * block
+    beside = plane + 1 - 2 * (plane % 2)
     with jax.named_scope("b1_left"):
         take(left_all, left_recv, plane % 2, place_left)
     with jax.named_scope("b2_near"):
-        take(right_all, right_recv, early * 2 + plane % 2, place_right)
+        take(right_all, right_recv, plane, place_right)
     with jax.named_scope("b3_left"):
         take(left_all, left_recv, 1 - plane % 2, place_left)
     with jax.named_scope("b4_lines"):
         for index in range(GROUP):
             left_lines[index] = channel(left_mat, index, 0, block_lines)
-    with jax.named_scope("c0_fin"):
-        finish(early * 2 + plane % 2)
-    with jax.named_scope("b5_far"):
-        take(right_all, right_recv, early * 2 + 1 - plane % 2, place_right)
-    with jax.named_scope("c1_fin"):
-        finish(early * 2 + 1 - plane % 2)
-    with jax.named_scope("c2_near"):
-        take(right_all, right_recv, 2 - block, place_right)
-    with jax.named_scope("c3_fin"):
-        finish(2 - block)
-    with jax.named_scope("c4_far"):
-        take(right_all, right_recv, 3 - 3 * block, place_right)
-    with jax.named_scope("c5_fin"):
-        finish(3 - 3 * block)
+    with jax.named_scope("b5_fin"):
+        finish(plane)
+    swap = outer * core
+    second = beside + swap * (across_inner - beside)
+    third = across_inner + swap * (beside - across_inner)
+    for index, which in enumerate((second, third, across_outer)):
+        with jax.named_scope(f"c{2 * index}_take"):
+            take(right_all, right_recv, which, place_right)
+        with jax.named_scope(f"c{2 * index + 1}_fin"):
+            finish(which)
     with jax.named_scope("d0_back"):
         all_of(owned, back_recv.at[0]).wait()
 

time: 25.4 us -> 25 us (0.984)
  Pallas kernels: 24.5 us -> 24.1 us
    pallas_call x1, Pallas kernels: 24.5 us -> 24.1 us  [fused(): pl.pallas_call(functools.partial(fused_kernel, sizes, pair_act.shape), ou...]
where the time goes in v6:
time: 25 us; the launch traced here: 24.9 us
  Pallas kernels  24.1 us (96%)
  local copies, waits for them, and re-layouts  0.72 us (3%)
    pallas_call x1, Pallas kernels, fused(): pl.pallas_call(functools.partial(fused_kernel, sizes, pair_act.shape), ou...  24.1 us
    unnamed x1, local copies, waits for them, and re-layouts  0.72 us

profile of v6, /device:TPU:0, one launch (start us, length us, event | category | flops | bytes accessed | tf_op | source)
XLA Modules:
  0.0 24.9 jit_solution(5827619131753434774)
XLA Ops:
  0.0 24.1 %shard_map.82 = bf16[12,96,128]{2,1,0:T(8,128)(2,1)S(1)} custom-call(bf16[4,3,3,32,128]{4,3,2,1,0:T(8,128)(2,1)} %bitcast.1, s32[12,12]{1,0:T(8,128)} %tiles_in.1, bf16[128,128]{1,0:T(8,128)(2,1)} %rest_0_.1, bf16[128,128]{1,0:T(8,128)(2,1)} %rest_1_.1, bf16[128,128]{1,0:T(8,128)(2,1)} %rest_2_.1, bf16[128,128]{1,0:T(8,128)(2,1)} %rest_3_.1, ...), custom_call_target="tpu_custom_call" | custom-call | tf_op jit(solution)/shard_map/pallas_call | solution.py:646
  24.1 0.7 %copy.10 = bf16[12,96,128]{2,1,0:T(8,128)(2,1)} copy(bf16[12,96,128]{2,1,0:T(8,128)(2,1)S(1)} %shard_map.82) | data formatting | bytes 589824

commit v7 on v6

--- a/solution.py
+++ b/solution.py
@@ -397,16 +397,27 @@
         def _():
             send_early(lows[3])
 
+        @pl.when(outer == 0)
+        def _():
+            send_across(lows[3], 0, to_inner)
+            send_across(lows[3], 1, to_outer)
+
     def send_level(low_flips, to_core):
         send_right(reach((0, 0, *low_flips), to_core))
         send_left(reach((0, 0, *low_flips), to_core))
 
     def send_mixed(low_flips):
-        @pl.when(outer == 1)
+        @pl.when(plane == 0)
         def _():
             send_lefts(low_flips)
             send_besides(low_flips)
             send_early(low_flips)
+
+        @pl.when(plane == 3)
+        def _():
+            send_lefts(low_flips)
+            send_early(low_flips)
+            send_besides(low_flips)
 
         @pl.when(outer == 0)
         def _():
@@ -447,9 +458,15 @@
             for low_flips in lows:
                 send_beside(low_flips, 1)
 
-        for low_flips in lows:
+        for low_flips in lows[:3]:
             send_across(low_flips, 0, to_inner)
             send_across(low_flips, 1, to_outer)
+
+        @pl.when(outer == 1)
+        def _():
+            send_across(lows[3], 0, to_inner)
+            send_across(lows[3], 1, to_outer)
+
         keep(left, left_all.at[member], left_recv.at[member // QUAD]).start()
         keep(right, right_all.at[flat], right_recv.at[own_quad]).start()
 

time: 25 us -> 24.7 us (0.988)
  Pallas kernels: 24.1 us -> 23.8 us
    pallas_call x1, Pallas kernels: 24.1 us -> 23.8 us  [fused(): pl.pallas_call(functools.partial(fused_kernel, sizes, pair_act.shape), ou...]
where the time goes in v7:
time: 24.7 us; the launch traced here: 24.5 us
  Pallas kernels  23.8 us (96%)
  local copies, waits for them, and re-layouts  0.72 us (3%)
    pallas_call x1, Pallas kernels, fused(): pl.pallas_call(functools.partial(fused_kernel, sizes, pair_act.shape), ou...  23.8 us
    unnamed x1, local copies, waits for them, and re-layouts  0.72 us

profile of v7, /device:TPU:0, one launch (start us, length us, event | category | flops | bytes accessed | tf_op | source)
XLA Modules:
  0.0 24.5 jit_solution(16705260951725440666)
XLA Ops:
  0.0 23.8 %shard_map.82 = bf16[12,96,128]{2,1,0:T(8,128)(2,1)S(1)} custom-call(bf16[4,3,3,32,128]{4,3,2,1,0:T(8,128)(2,1)} %bitcast.1, s32[12,12]{1,0:T(8,128)} %tiles_in.1, bf16[128,128]{1,0:T(8,128)(2,1)} %rest_0_.1, bf16[128,128]{1,0:T(8,128)(2,1)} %rest_1_.1, bf16[128,128]{1,0:T(8,128)(2,1)} %rest_2_.1, bf16[128,128]{1,0:T(8,128)(2,1)} %rest_3_.1, ...), custom_call_target="tpu_custom_call" | custom-call | tf_op jit(solution)/shard_map/pallas_call | solution.py:663
  23.8 0.7 %copy.10 = bf16[12,96,128]{2,1,0:T(8,128)(2,1)} copy(bf16[12,96,128]{2,1,0:T(8,128)(2,1)S(1)} %shard_map.82) | data formatting | bytes 589824

commit v8 on v7

--- a/solution.py
+++ b/solution.py
@@ -227,12 +227,12 @@
 
 
 def fused_kernel(sizes, shape, pair_in, tiles_in, *rest):
-    weights_in, out = rest[:6], rest[6]
+    weights_in, (owned, gate, weights) = rest[:6], rest[6:9]
     (
-        pair, tiles, weights, pair_sem, input_sem,
-        normed, gate, left, right, left_all, right_all, left_mat, right_mat, left_lines, product, triangle, owned,
+        pair, tiles, pair_sem, input_sem,
+        normed, left, right, left_all, right_all, left_mat, right_mat, left_lines, product, triangle,
         send, left_recv, right_recv, back_recv, heard,
-    ) = rest[7:]
+    ) = rest[9:]
     row_size, col_size, groups = sizes
     rows, cols, width = shape
     devices = row_size * col_size
@@ -620,33 +620,47 @@
     with jax.named_scope("d0_back"):
         all_of(owned, back_recv.at[0]).wait()
 
-    with jax.named_scope("d1_out"):
-        for side, at in [(side, at) for side in range(2) for at in range(tiles_back)]:
-            piece = jnp.concatenate(
-                [
-                    owned[group, side, :, at * LANES : (at + 1) * LANES].astype(jnp.float32)
-                    for group in range(groups)
-                ],
-                axis=0,
-            )
-            scaled = norm_axis(piece, 0).T.astype(jnp.bfloat16)
-            projected = jnp.dot(scaled, weights[5], preferred_element_type=jnp.float32)
-            base = side * part
-            spots = [(2 * at, base, 0, part), (2 * at + 1, base, part, part)]
-            if at < 2:
-                spots.append((rows - 2 + at, base, cols, spare))
-            if at == 2:
-                rest = part - spare
-                spots.append((rows - 2, base + spare, cols, rest))
-                spots.append((rows - 1, base + spare, cols + rest, rest))
-            for line, start, begin, length in spots:
-                stop = start + length
-                made = gate[line, start:stop] * projected[begin : begin + length]
-                out[line, start:stop] = made.astype(jnp.bfloat16)
     with jax.named_scope("d2_sent"):
         all_of(right_all.at[pl.ds(0, devices - 1)], send.at[0]).wait()
         all_of(left_all.at[pl.ds(0, groups - 1)], send.at[1]).wait()
         all_of(triangle.at[pl.ds(0, groups - 1)], send.at[2]).wait()
+
+
+def close_kernel(owned, gate, weights, out, made_out, sem):
+    groups = owned.shape[0]
+    rows, cols, width = gate.shape
+    spare = LANES - cols
+    part = cols // 2
+    tiles_back = rows // 2 - 1
+    for side, at in [(side, at) for side in range(2) for at in range(tiles_back)]:
+        piece = jnp.concatenate(
+            [
+                owned[group, side, :, at * LANES : (at + 1) * LANES].astype(jnp.float32)
+                for group in range(groups)
+            ],
+            axis=0,
+        )
+        scaled = norm_axis(piece, 0).T.astype(jnp.bfloat16)
+        projected = jnp.dot(scaled, weights[5], preferred_element_type=jnp.float32)
+        base = side * part
+        spots = [(2 * at, base, 0, part), (2 * at + 1, base, part, part)]
+        if at < 2:
+            spots.append((rows - 2 + at, base, cols, spare))
+        if at == 2:
+            rest = part - spare
+            spots.append((rows - 2, base + spare, cols, rest))
+            spots.append((rows - 1, base + spare, cols + rest, rest))
+        for line, start, begin, length in spots:
+            stop = start + length
+            made = gate[line, start:stop] * projected[begin : begin + length]
+            made_out[line, start:stop] = made.astype(jnp.bfloat16)
+        lines = [(2 * at, 2)]
+        if at == 2:
+            lines.append((rows - 2, 2))
+        for line, length in lines:
+            piece = (pl.ds(line, length), pl.ds(base, part))
+            pltpu.make_async_copy(made_out.at[piece], out.at[piece], sem).start()
+    pltpu.make_async_copy(made_out, made_out, sem).wait()
 
 
 def fused(sizes, pair_act, tile_mask, *weights):
@@ -660,19 +674,22 @@
     dma = pltpu.SemaphoreType.DMA
     chunks = pltpu.VMEM((groups, GROUP, pairs), jnp.bfloat16)
     parts = pltpu.VMEM((groups, 2, GROUP, (rows // 2 - 1) * LANES), jnp.bfloat16)
-    result = pl.pallas_call(
+    kept = pl.BlockSpec(memory_space=pltpu.VMEM)
+    results = pl.pallas_call(
         functools.partial(fused_kernel, sizes, pair_act.shape),
-        out_shape=pltpu.VMEM((rows, cols, width), jnp.bfloat16),
+        out_shape=(
+            parts,
+            pltpu.VMEM((rows, cols, width), jnp.float32),
+            pltpu.VMEM((6, width, width), jnp.bfloat16),
+        ),
         in_specs=[pl.BlockSpec(memory_space=pltpu.HBM)] * 8,
-        out_specs=pl.BlockSpec(memory_space=pltpu.VMEM),
+        out_specs=(kept, kept, kept),
         scratch_shapes=[
             pltpu.VMEM((extra, extra, extra + 1, spare, width), jnp.bfloat16),
             pltpu.VMEM(tile_mask.shape, tile_mask.dtype),
-            pltpu.VMEM((6, width, width), jnp.bfloat16),
             dma((1,)),
             dma((2,)),
             pltpu.VMEM((pairs, width), jnp.bfloat16),
-            pltpu.VMEM((rows, cols, width), jnp.float32),
             chunks,
             chunks,
             chunks,
@@ -682,7 +699,6 @@
             pltpu.VMEM((GROUP, block_rows * rows, col_size * LANES), jnp.bfloat16),
             pltpu.VMEM((block_rows * rows * GROUP, LANES), jnp.float32),
             parts,
-            parts,
             dma((3,)),
             dma((groups // QUAD,)),
             dma((devices // QUAD,)),
@@ -691,7 +707,13 @@
         ],
         compiler_params=pltpu.CompilerParams(collective_id=2, has_side_effects=True),
     )(pair_act.reshape(extra + 1, extra, extra, spare, width), tile_mask, *weights)
-    return result
+    return pl.pallas_call(
+        close_kernel,
+        out_shape=jax.ShapeDtypeStruct((rows, cols, width), jnp.bfloat16),
+        in_specs=[kept] * 3,
+        out_specs=pl.BlockSpec(memory_space=pltpu.HBM),
+        scratch_shapes=[pltpu.VMEM((rows, cols, width), jnp.bfloat16), pltpu.SemaphoreType.DMA],
+    )(*[pltpu.with_memory_space_constraint(array, pltpu.VMEM) for array in results])
 
 
 def fits(sizes, rows, cols):

time: 24.7 us -> 24.6 us (level)
  local copies, waits for them, and re-layouts: 0.72 us -> 0 us
  Pallas kernels: 23.8 us -> 24.5 us
    pallas_call x0 -> x1, Pallas kernels: none -> 1.06 us  [fused(): pl.pallas_call(close_kernel, out_shape=jax.ShapeDtypeStruct((rows, cols,...]
    unnamed x1 -> x0, local copies, waits for them, and re-layouts: 0.72 us -> none
    pallas_call x1, Pallas kernels: 23.8 us -> 23.4 us  [fused(): pl.pallas_call(functools.partial(fused_kernel, sizes, pair_act.shape), ou...]
where the time goes in v8:
time: 24.6 us; the launch traced here: 24.5 us
  Pallas kernels  24.5 us (100%)
    pallas_call x1, Pallas kernels, fused(): pl.pallas_call(functools.partial(fused_kernel, sizes, pair_act.shape), ou...  23.4 us
    pallas_call x1, Pallas kernels, fused(): pl.pallas_call(close_kernel, out_shape=jax.ShapeDtypeStruct((rows, cols,...  1.06 us

profile of v8, /device:TPU:0, one launch (start us, length us, event | category | flops | bytes accessed | tf_op | source)
XLA Modules:
  0.0 24.5 jit_solution(1930789924010140022)
XLA Ops:
  0.0 23.4 %shard_map.82 = (bf16[16,2,8,640]{3,2,1,0:T(8,128)(2,1)S(1)}, f32[12,96,128]{2,1,0:T(8,128)S(1)}, bf16[6,128,128]{2,1,0:T(8,128)(2,1)S(1)}) custom-call(bf16[4,3,3,32,128]{4,3,2,1,0:T(8,128)(2,1)} %bitcast.1, s32[12,12]{1,0:T(8,128)} %tiles_in.1, bf16[128,128]{1,0:T(8,128)(2,1)} %rest_0_.1, bf16[128,128]{1,0:T(8,128)(2,1)} %rest_1_.1, ...), custom_call_target="tpu_custom_call" | custom-call | tf_op jit(solution)/shard_map/pallas_call | solution.py:678
  23.4 1.1 %shard_map.83 = bf16[12,96,128]{2,1,0:T(8,128)(2,1)} custom-call(bf16[16,2,8,640]{3,2,1,0:T(8,128)(2,1)S(1)} %get-tuple-element.8.owned, f32[12,96,128]{2,1,0:T(8,128)S(1)} %get-tuple-element.9.gate, bf16[6,128,128]{2,1,0:T(8,128)(2,1)S(1)} %get-tuple-element.10.weights), custom_call_target="tpu_custom_call" | custom-call | tf_op jit(solution)/shard_map/pallas_call | solution.py:710
